TPU v7x, 32 devices: a whole 2x2x4 slice. The times are simulated.
32 devices in a mesh: beta: 16 (over z, y, x), grp: 2 (over core).
Axes of the slice: x: 2, y: 2, z: 4, core: 2. Of those that a mesh axis runs over, the one named last changes fastest.
Arguments:
- samples: float32 [128, 8, 128, 128], P('beta', 'grp'), parts along dimension 1, may hold values from -6 to 6
Outputs:
- coeffs: float32 [128, 2, 8, 64, 64], P('beta', None, 'grp'), parts along dimension 2
- power: float32 [8, 64], P('grp'), parts along dimension 0
There are 2 independent parts, one for each index of `grp`. A program takes and returns all parts, laid end to end along the dimension named above; each array names one. Nothing has to cross between parts.
All inputs are finite; a program needn't handle non-finite values.
Results may differ from a plain program's by a relative error of at most 0.0003.
Values sent between devices are 32-bit elements; how exact they have to be, the bound alone decides.
No kernel may reach another device: no remote copies, remote signals or barrier semaphores. Data moves between devices by JAX's collectives and lax.ppermute only.
A program may use at most 64 MiB of HBM per device.

v0:
```python
import jax
import jax.numpy as jnp
from jax import lax
from jax.sharding import PartitionSpec as P

HIGHEST = lax.Precision.HIGHEST


def beta_angles(spread):
    grid_size = 2 * spread
    return (2.0 * jnp.arange(grid_size, dtype=jnp.float32) + 1.0) * (jnp.pi / (4.0 * spread))


def quadrature(spread):
    angles = beta_angles(spread)
    odd_terms = 2.0 * jnp.arange(spread, dtype=jnp.float32) + 1.0
    series = jnp.sum(jnp.sin(angles[:, None] * odd_terms[None, :]) / odd_terms[None, :], axis=1)
    return 2.0 / spread * jnp.sin(angles) * series


def gamma_table(spread):
    grid_size = 2 * spread
    positions = jnp.arange(grid_size, dtype=jnp.int32)
    orders = jnp.arange(spread, dtype=jnp.int32)
    phase_index = positions[:, None] * orders[None, :] % grid_size
    angles = phase_index.astype(jnp.float32) * (2.0 * jnp.pi / grid_size)
    return jnp.concatenate([jnp.cos(angles), -jnp.sin(angles)], axis=1)


def alpha_table(spread, row_index):
    grid_size = 2 * spread
    positions = jnp.arange(grid_size, dtype=jnp.int32)
    phase_index = row_index[:, None] * positions[None, :] % grid_size
    angles = phase_index.astype(jnp.float32) * (2.0 * jnp.pi / grid_size)
    cosine = jnp.cos(angles) / grid_size
    sine_part = jnp.sin(angles) / grid_size
    real_rows = jnp.stack([cosine, sine_part], axis=1)
    imag_rows = jnp.stack([-sine_part, cosine], axis=1)
    return jnp.stack([real_rows, imag_rows], axis=0)


def log_factorial(value, float_type):
    return lax.lgamma((value + 1).astype(float_type))


def wigner_start(alpha_order, gamma_order, log_cosine, log_sine):
    float_type = log_cosine.dtype
    lowest = jnp.maximum(jnp.abs(alpha_order), gamma_order)
    shift_low = jnp.maximum(0, gamma_order - alpha_order)
    magnitude = 0.5 * (
        log_factorial(lowest + alpha_order, float_type)
        + log_factorial(lowest - alpha_order, float_type)
        + log_factorial(lowest + gamma_order, float_type)
        + log_factorial(lowest - gamma_order, float_type)
    )
    magnitude = (
        magnitude
        - log_factorial(lowest + gamma_order - shift_low, float_type)
        - log_factorial(shift_low, float_type)
    )
    magnitude = magnitude - log_factorial(alpha_order - gamma_order + shift_low, float_type)
    magnitude = magnitude - log_factorial(lowest - alpha_order - shift_low, float_type)
    cos_power = (2 * lowest + gamma_order - alpha_order - 2 * shift_low).astype(float_type)
    sin_power = (alpha_order - gamma_order + 2 * shift_low).astype(float_type)
    parity = (alpha_order - gamma_order + shift_low) % 2
    sign_factor = (1 - 2 * parity).astype(float_type)
    return sign_factor * jnp.exp(magnitude + cos_power * log_cosine + sin_power * log_sine)


def advance(degree, carried, alpha_order, gamma_order, cos_angles, start_value, lowest):
    former, current = carried
    float_type = current.dtype
    previous = (degree - 1).astype(float_type)
    alpha_float = alpha_order.astype(float_type)
    gamma_float = gamma_order.astype(float_type)
    cross_ratio = alpha_float * gamma_float / jnp.maximum(previous * (previous + 1.0), 1.0)
    upper_term = ((previous + 1.0) * (previous + 1.0) - alpha_float * alpha_float) * (
        (previous + 1.0) * (previous + 1.0) - gamma_float * gamma_float
    )
    lower_term = (previous * previous - alpha_float * alpha_float) * (
        previous * previous - gamma_float * gamma_float
    )
    root_upper = jnp.sqrt(jnp.maximum(upper_term, 1.0))
    forward = (previous + 1.0) * (2.0 * previous + 1.0) / root_upper
    backward = (
        (previous + 1.0)
        * jnp.sqrt(jnp.maximum(lower_term, 0.0))
        / (jnp.maximum(previous, 1.0) * root_upper)
    )
    recurred = forward * (cos_angles - cross_ratio) * current - backward * former
    renewed = jnp.where(degree == lowest, start_value, recurred)
    return (current, renewed)


def degree_rows(row_index, weighted, spread):
    stride = 8
    grid_size = 2 * spread
    group_size = row_index.shape[0]
    channels = weighted.shape[2]
    block_count = spread // stride
    alpha_order = jnp.where(row_index < spread, row_index, row_index - grid_size)[:, None, None]
    gamma_order = jnp.arange(spread, dtype=jnp.int32)[None, None, :]
    angles = beta_angles(spread)
    cos_angles = jnp.cos(angles)[None, :, None]
    log_cosine = jnp.log(jnp.cos(0.5 * angles))[None, :, None]
    log_sine = jnp.log(jnp.sin(0.5 * angles))[None, :, None]
    lowest = jnp.maximum(jnp.abs(alpha_order), gamma_order)
    start_value = wigner_start(alpha_order, gamma_order, log_cosine, log_sine)
    first_block = jnp.min(jnp.abs(alpha_order)) // stride
    empty_state = jnp.zeros((group_size, grid_size, spread), jnp.float32)

    def compute_block(operands):
        block_index, former, current = operands
        levels = []
        for offset in range(stride):
            former, current = advance(
                block_index * stride + offset,
                (former, current),
                alpha_order,
                gamma_order,
                cos_angles,
                start_value,
                lowest,
            )
            levels.append(current)
        stacked = jnp.stack(levels, axis=0)
        block_part = jnp.einsum("jgkq,kgcq->gcjq", stacked, weighted, precision=HIGHEST)
        return (former, current, block_part)

    def skip_block(operands):
        block_index, former, current = operands
        return (former, current, jnp.zeros((group_size, channels, stride, spread), jnp.float32))

    def block_step(carried, block_index):
        former, current = carried
        former, current, block_part = lax.cond(
            block_index >= first_block, compute_block, skip_block, (block_index, former, current)
        )
        return ((former, current), block_part)

    _, parts = lax.scan(
        block_step, (empty_state, empty_state), jnp.arange(block_count, dtype=jnp.int32)
    )
    output = jnp.transpose(parts, (1, 2, 0, 3, 4)).reshape(group_size, channels, spread, spread)
    degree_scale = 8.0 * jnp.sqrt(2.0 * jnp.arange(spread, dtype=jnp.float32) + 1.0)
    return output * degree_scale[None, None, :, None]


def degree_energy(coeffs, functions, spread):
    split_view = coeffs.reshape(coeffs.shape[0], 2, functions, spread, spread)
    multiplicity = jnp.where(jnp.arange(spread) == 0, 1.0, 2.0).astype(jnp.float32)
    energy_sum = jnp.sum(split_view * split_view * multiplicity, axis=(0, 1, 4))
    degrees = 2.0 * jnp.arange(spread, dtype=jnp.float32) + 1.0
    return energy_sum / (degrees * degrees)[None, :]


def local(samples):
    devices = lax.axis_size("beta")
    device = lax.axis_index("beta")
    local_beta = samples.shape[0]
    functions = samples.shape[1]
    grid_size = samples.shape[2]
    spread = grid_size // 2
    channels = 2 * functions
    row_count = grid_size // devices
    natural_rows = jnp.arange(grid_size, dtype=jnp.int32)
    halfway = jnp.einsum("kfag,gx->kfax", samples, gamma_table(spread), precision=HIGHEST)
    halfway = halfway.reshape(local_beta, functions, grid_size, 2, spread)
    spectrum = jnp.einsum(
        "kfacq,spca->kpsfq", halfway, alpha_table(spread, natural_rows), precision=HIGHEST
    )
    spectrum = spectrum.reshape(local_beta, grid_size, channels, spread)
    received = lax.all_to_all(spectrum, "beta", split_axis=1, concat_axis=0, tiled=True)
    weighted = received * quadrature(spread)[:, None, None, None]
    owned_rows = lax.dynamic_slice_in_dim(natural_rows, device * row_count, row_count)
    computed = degree_rows(owned_rows, weighted, spread)
    power_part = degree_energy(computed, functions, spread)
    coeffs = computed
    power = lax.psum(power_part, "beta")
    coeffs = coeffs.reshape(row_count, 2, functions, spread, spread)
    return (coeffs, power)


def solution(mesh):
    return jax.shard_map(
        local,
        mesh=mesh,
        in_specs=(P("beta", "grp", None, None),),
        out_specs=(P("beta", None, "grp", None, None), P("grp", None)),
        check_vma=False,
    )
```

profile of v0, /device:TPU:0, one launch (start us, length us, event | category | flops | bytes accessed | tf_op | source)
XLA Modules:
  0.0 345.6 jit_solution(5608972519271680303)
XLA Ops:
  7.7 5.6 %copy.58 = f32[8,128,8,64]{3,2,0,1:T(8,128)} copy(f32[8,128,8,64]{1,3,2,0:T(8,128)} %bitcast.233) | data formatting | bytes 4194304 | tf_op jit(solution)/shard_map/reshape | solution.py:172
  13.3 5.5 %reshape.2457 = f32[16,1,32768]{2,1,0:T(1,128)} reshape(f32[128,8,8,64]{3,2,1,0:T(8,128)} %bitcast.230) | data formatting | bytes 4194304
  18.8 8.4 %all-to-all-start = ((f32[16,1,32768]{2,1,0:T(1,128)}), f32[16,1,32768]{2,1,0:T(1,128)}, u32[]{:S(2)}, u32[]{:S(2)}) async-start(f32[16,1,32768]{2,1,0:T(1,128)} %reshape.2457), calls=%async_computation | async-start | bytes 4194304 | tf_op jit(solution)/shard_map/all_to_all | solution.py:173
  32.1 38.1 %all-to-all-done = f32[16,1,32768]{2,1,0:T(1,128)} async-done(((f32[16,1,32768]{2,1,0:T(1,128)}), f32[16,1,32768]{2,1,0:T(1,128)}, u32[]{:S(2)}, u32[]{:S(2)}) %all-to-all-start) | async-done | bytes 2097184 | tf_op jit(solution)/shard_map/all_to_all | solution.py:173
  70.9 8.6 %reduce.3 = f32[16,32768]{1,0:T(8,128)} reduce(f32[16,1,32768]{2,1,0:T(1,128)} %all-to-all-done, f32[]{:T(128)} %broadcast.2681), dimensions={1}, to_apply=%all_to_all.13.reduce_sub_computation | reduce | bytes 4194308 | tf_op jit(solution)/shard_map/all_to_all | solution.py:173
  79.5 4.2 %reshape.2458 = f32[128,8,8,64]{3,2,1,0:T(8,128)} reshape(f32[16,32768]{1,0:T(8,128)} %reduce.3) | data formatting | bytes 4194304
  88.8 5.0 %copy.61 = f32[128,8,8,64]{0,2,3,1:T(8,128)} copy(f32[128,8,8,64]{3,2,1,0:T(8,128)} %bitcast_multiply_fusion) | data formatting | bytes 4194304
  93.9 182.8 %while.16 = (s32[]{:T(128)}, f32[8,128,64]{1,2,0:T(8,128)S(1)}, f32[8,128,64]{1,2,0:T(8,128)S(1)}, f32[8,8,8,8,64]{2,3,4,1,0:T(8,128)}, s32[8]{0:T(128)S(1)}, /*...) while((s32[]{:T(128)}, f32[8,128,64]{1,2,0:T(8,128)S(1)}, ...), condition=%wide.region_5.6_spmd.clone.clone, body=%wide.region_2.5_spmd.clone.clone.sunk | while | flops 53850804 | bytes 15474387 | solution.py:141
  95.2 18.6 %conditional.4 = (f32[8,128,64]{1,2,0:T(8,128)S(1)}, f32[8,128,64]{1,2,0:T(8,128)S(1)}, f32[1,8,8,8,64]{2,3,4,1,0:T(8,128)}) conditional(s32[]{:T(128)} %convert_element_type.412, (f32[8,128,64]{1,2,0:T(8,128)S(1)}, f32[8,128,64]{1,2,0:T(8,128)S(1)}) %tuple.139, (s32[]{:T(128)}, s32[8]{0:T(128)S(1)}, s32[8,1,1]{0,2,1:T(1,128)S(1)}, ...), branch_computations={%region_3.3_spmd, %region_4.4_spmd.clone} | conditional | flops 53850800 | bytes 11276004 | solution.py:136
  97.1 3.6 %fusion.11 = (f32[8,128,64]{1,2,0:T(8,128)S(1)}, f32[8,128,64]{1,2,0:T(8,128)S(1)}, f32[8,128,64]{1,2,0:T(8,128)S(1)}, f32[8,128,64]{1,2,0:T(8,128)S(1)}, f32[8,...) fusion(f32[128]{0:T(128)S(1)} %get-tuple-element.437, ...), kind=kLoop, calls=%fused_computation.9 | loop fusion | flops 3473408 | bytes 2684416 | tf_op jit(solution)/shard_map/while/body/eval_jaxpr/cond/branch_1_fun/jit(_where)/select_n | solution.py:91
  100.7 6.2 %stack.51 = f32[8,8,128,64]{2,0,3,1:T(8,128)} concatenate(f32[1,8,128,64]{2,0,3,1:T(1,128)} %bitcast.229, f32[1,8,128,64]{2,0,3,1:T(1,128)} %bitcast.228, f32[1,8,128,64]{2,0,3,1:T(1,128)} %bitcast.227, f32[1,8,128,64]{2,0,3,1:T(1,128)S(1)} %bitcast.226, f32[1,8,128,64]{2,0,3,1:T(1,128)S(1)} %bitcast.225, f32[1,8,128,64]{2,0,3,1:T(1,128)S(1)} %bitcast.224, ...), dimensions={0} | concatenate | bytes 4194304 | tf_op jit(solution)/shard_map/while/body/eval_jaxpr/cond/branch_1_fun/stack | solution.py:126
  106.9 6.9 %convolution_bitcast_fusion = f32[1,8,8,8,64]{2,3,4,1,0:T(8,128)} fusion(f32[8,8,128,64]{2,0,3,1:T(8,128)} %stack.51, f32[128,8,8,64]{0,2,3,1:T(8,128)} %get-tuple-element.428), kind=kOutput, calls=%fused_computation.4 | convolution fusion | flops 50331648 | bytes 4325376 | tf_op jit(solution)/shard_map/while/body/eval_jaxpr/cond/branch_1_fun/jgkq,kgcq->gcjq/dot_general | solution.py:127
  118.1 18.6 %conditional.4 = (f32[8,128,64]{1,2,0:T(8,128)S(1)}, f32[8,128,64]{1,2,0:T(8,128)S(1)}, f32[1,8,8,8,64]{2,3,4,1,0:T(8,128)}) conditional(s32[]{:T(128)} %convert_element_type.412, (f32[8,128,64]{1,2,0:T(8,128)S(1)}, f32[8,128,64]{1,2,0:T(8,128)S(1)}) %tuple.139, (s32[]{:T(128)}, s32[8]{0:T(128)S(1)}, s32[8,1,1]{0,2,1:T(1,128)S(1)}, ...), branch_computations={%region_3.3_spmd, %region_4.4_spmd.clone} | conditional | flops 53850800 | bytes 11276004 | solution.py:136
  119.9 3.6 %fusion.11 = (f32[8,128,64]{1,2,0:T(8,128)S(1)}, f32[8,128,64]{1,2,0:T(8,128)S(1)}, f32[8,128,64]{1,2,0:T(8,128)S(1)}, f32[8,128,64]{1,2,0:T(8,128)S(1)}, f32[8,...) fusion(f32[128]{0:T(128)S(1)} %get-tuple-element.437, ...), kind=kLoop, calls=%fused_computation.9 | loop fusion | flops 3473408 | bytes 2684416 | tf_op jit(solution)/shard_map/while/body/eval_jaxpr/cond/branch_1_fun/jit(_where)/select_n | solution.py:91
  123.5 6.2 %stack.51 = f32[8,8,128,64]{2,0,3,1:T(8,128)} concatenate(f32[1,8,128,64]{2,0,3,1:T(1,128)} %bitcast.229, f32[1,8,128,64]{2,0,3,1:T(1,128)} %bitcast.228, f32[1,8,128,64]{2,0,3,1:T(1,128)} %bitcast.227, f32[1,8,128,64]{2,0,3,1:T(1,128)S(1)} %bitcast.226, f32[1,8,128,64]{2,0,3,1:T(1,128)S(1)} %bitcast.225, f32[1,8,128,64]{2,0,3,1:T(1,128)S(1)} %bitcast.224, ...), dimensions={0} | concatenate | bytes 4194304 | tf_op jit(solution)/shard_map/while/body/eval_jaxpr/cond/branch_1_fun/stack | solution.py:126
  129.7 6.9 %convolution_bitcast_fusion = f32[1,8,8,8,64]{2,3,4,1,0:T(8,128)} fusion(f32[8,8,128,64]{2,0,3,1:T(8,128)} %stack.51, f32[128,8,8,64]{0,2,3,1:T(8,128)} %get-tuple-element.428), kind=kOutput, calls=%fused_computation.4 | convolution fusion | flops 50331648 | bytes 4325376 | tf_op jit(solution)/shard_map/while/body/eval_jaxpr/cond/branch_1_fun/jgkq,kgcq->gcjq/dot_general | solution.py:127
  140.9 18.6 %conditional.4 = (f32[8,128,64]{1,2,0:T(8,128)S(1)}, f32[8,128,64]{1,2,0:T(8,128)S(1)}, f32[1,8,8,8,64]{2,3,4,1,0:T(8,128)}) conditional(s32[]{:T(128)} %convert_element_type.412, (f32[8,128,64]{1,2,0:T(8,128)S(1)}, f32[8,128,64]{1,2,0:T(8,128)S(1)}) %tuple.139, (s32[]{:T(128)}, s32[8]{0:T(128)S(1)}, s32[8,1,1]{0,2,1:T(1,128)S(1)}, ...), branch_computations={%region_3.3_spmd, %region_4.4_spmd.clone} | conditional | flops 53850800 | bytes 11276004 | solution.py:136
  142.7 3.6 %fusion.11 = (f32[8,128,64]{1,2,0:T(8,128)S(1)}, f32[8,128,64]{1,2,0:T(8,128)S(1)}, f32[8,128,64]{1,2,0:T(8,128)S(1)}, f32[8,128,64]{1,2,0:T(8,128)S(1)}, f32[8,...) fusion(f32[128]{0:T(128)S(1)} %get-tuple-element.437, ...), kind=kLoop, calls=%fused_computation.9 | loop fusion | flops 3473408 | bytes 2684416 | tf_op jit(solution)/shard_map/while/body/eval_jaxpr/cond/branch_1_fun/jit(_where)/select_n | solution.py:91
  146.3 6.2 %stack.51 = f32[8,8,128,64]{2,0,3,1:T(8,128)} concatenate(f32[1,8,128,64]{2,0,3,1:T(1,128)} %bitcast.229, f32[1,8,128,64]{2,0,3,1:T(1,128)} %bitcast.228, f32[1,8,128,64]{2,0,3,1:T(1,128)} %bitcast.227, f32[1,8,128,64]{2,0,3,1:T(1,128)S(1)} %bitcast.226, f32[1,8,128,64]{2,0,3,1:T(1,128)S(1)} %bitcast.225, f32[1,8,128,64]{2,0,3,1:T(1,128)S(1)} %bitcast.224, ...), dimensions={0} | concatenate | bytes 4194304 | tf_op jit(solution)/shard_map/while/body/eval_jaxpr/cond/branch_1_fun/stack | solution.py:126
  152.5 6.9 %convolution_bitcast_fusion = f32[1,8,8,8,64]{2,3,4,1,0:T(8,128)} fusion(f32[8,8,128,64]{2,0,3,1:T(8,128)} %stack.51, f32[128,8,8,64]{0,2,3,1:T(8,128)} %get-tuple-element.428), kind=kOutput, calls=%fused_computation.4 | convolution fusion | flops 50331648 | bytes 4325376 | tf_op jit(solution)/shard_map/while/body/eval_jaxpr/cond/branch_1_fun/jgkq,kgcq->gcjq/dot_general | solution.py:127
  159.5 3.1 constant_dynamic-update-slice_fusion.2
  163.7 18.6 %conditional.4 = (f32[8,128,64]{1,2,0:T(8,128)S(1)}, f32[8,128,64]{1,2,0:T(8,128)S(1)}, f32[1,8,8,8,64]{2,3,4,1,0:T(8,128)}) conditional(s32[]{:T(128)} %convert_element_type.412, (f32[8,128,64]{1,2,0:T(8,128)S(1)}, f32[8,128,64]{1,2,0:T(8,128)S(1)}) %tuple.139, (s32[]{:T(128)}, s32[8]{0:T(128)S(1)}, s32[8,1,1]{0,2,1:T(1,128)S(1)}, ...), branch_computations={%region_3.3_spmd, %region_4.4_spmd.clone} | conditional | flops 53850800 | bytes 11276004 | solution.py:136
  165.5 3.6 %fusion.11 = (f32[8,128,64]{1,2,0:T(8,128)S(1)}, f32[8,128,64]{1,2,0:T(8,128)S(1)}, f32[8,128,64]{1,2,0:T(8,128)S(1)}, f32[8,128,64]{1,2,0:T(8,128)S(1)}, f32[8,...) fusion(f32[128]{0:T(128)S(1)} %get-tuple-element.437, ...), kind=kLoop, calls=%fused_computation.9 | loop fusion | flops 3473408 | bytes 2684416 | tf_op jit(solution)/shard_map/while/body/eval_jaxpr/cond/branch_1_fun/jit(_where)/select_n | solution.py:91
  169.1 6.2 %stack.51 = f32[8,8,128,64]{2,0,3,1:T(8,128)} concatenate(f32[1,8,128,64]{2,0,3,1:T(1,128)} %bitcast.229, f32[1,8,128,64]{2,0,3,1:T(1,128)} %bitcast.228, f32[1,8,128,64]{2,0,3,1:T(1,128)} %bitcast.227, f32[1,8,128,64]{2,0,3,1:T(1,128)S(1)} %bitcast.226, f32[1,8,128,64]{2,0,3,1:T(1,128)S(1)} %bitcast.225, f32[1,8,128,64]{2,0,3,1:T(1,128)S(1)} %bitcast.224, ...), dimensions={0} | concatenate | bytes 4194304 | tf_op jit(solution)/shard_map/while/body/eval_jaxpr/cond/branch_1_fun/stack | solution.py:126
  175.3 6.9 %convolution_bitcast_fusion = f32[1,8,8,8,64]{2,3,4,1,0:T(8,128)} fusion(f32[8,8,128,64]{2,0,3,1:T(8,128)} %stack.51, f32[128,8,8,64]{0,2,3,1:T(8,128)} %get-tuple-element.428), kind=kOutput, calls=%fused_computation.4 | convolution fusion | flops 50331648 | bytes 4325376 | tf_op jit(solution)/shard_map/while/body/eval_jaxpr/cond/branch_1_fun/jgkq,kgcq->gcjq/dot_general | solution.py:127
  182.3 3.1 constant_dynamic-update-slice_fusion.2
  186.5 18.6 %conditional.4 = (f32[8,128,64]{1,2,0:T(8,128)S(1)}, f32[8,128,64]{1,2,0:T(8,128)S(1)}, f32[1,8,8,8,64]{2,3,4,1,0:T(8,128)}) conditional(s32[]{:T(128)} %convert_element_type.412, (f32[8,128,64]{1,2,0:T(8,128)S(1)}, f32[8,128,64]{1,2,0:T(8,128)S(1)}) %tuple.139, (s32[]{:T(128)}, s32[8]{0:T(128)S(1)}, s32[8,1,1]{0,2,1:T(1,128)S(1)}, ...), branch_computations={%region_3.3_spmd, %region_4.4_spmd.clone} | conditional | flops 53850800 | bytes 11276004 | solution.py:136
  188.4 3.6 %fusion.11 = (f32[8,128,64]{1,2,0:T(8,128)S(1)}, f32[8,128,64]{1,2,0:T(8,128)S(1)}, f32[8,128,64]{1,2,0:T(8,128)S(1)}, f32[8,128,64]{1,2,0:T(8,128)S(1)}, f32[8,...) fusion(f32[128]{0:T(128)S(1)} %get-tuple-element.437, ...), kind=kLoop, calls=%fused_computation.9 | loop fusion | flops 3473408 | bytes 2684416 | tf_op jit(solution)/shard_map/while/body/eval_jaxpr/cond/branch_1_fun/jit(_where)/select_n | solution.py:91
  191.9 6.2 %stack.51 = f32[8,8,128,64]{2,0,3,1:T(8,128)} concatenate(f32[1,8,128,64]{2,0,3,1:T(1,128)} %bitcast.229, f32[1,8,128,64]{2,0,3,1:T(1,128)} %bitcast.228, f32[1,8,128,64]{2,0,3,1:T(1,128)} %bitcast.227, f32[1,8,128,64]{2,0,3,1:T(1,128)S(1)} %bitcast.226, f32[1,8,128,64]{2,0,3,1:T(1,128)S(1)} %bitcast.225, f32[1,8,128,64]{2,0,3,1:T(1,128)S(1)} %bitcast.224, ...), dimensions={0} | concatenate | bytes 4194304 | tf_op jit(solution)/shard_map/while/body/eval_jaxpr/cond/branch_1_fun/stack | solution.py:126
  198.2 6.9 %convolution_bitcast_fusion = f32[1,8,8,8,64]{2,3,4,1,0:T(8,128)} fusion(f32[8,8,128,64]{2,0,3,1:T(8,128)} %stack.51, f32[128,8,8,64]{0,2,3,1:T(8,128)} %get-tuple-element.428), kind=kOutput, calls=%fused_computation.4 | convolution fusion | flops 50331648 | bytes 4325376 | tf_op jit(solution)/shard_map/while/body/eval_jaxpr/cond/branch_1_fun/jgkq,kgcq->gcjq/dot_general | solution.py:127
  205.1 3.1 constant_dynamic-update-slice_fusion.2
  209.4 18.6 %conditional.4 = (f32[8,128,64]{1,2,0:T(8,128)S(1)}, f32[8,128,64]{1,2,0:T(8,128)S(1)}, f32[1,8,8,8,64]{2,3,4,1,0:T(8,128)}) conditional(s32[]{:T(128)} %convert_element_type.412, (f32[8,128,64]{1,2,0:T(8,128)S(1)}, f32[8,128,64]{1,2,0:T(8,128)S(1)}) %tuple.139, (s32[]{:T(128)}, s32[8]{0:T(128)S(1)}, s32[8,1,1]{0,2,1:T(1,128)S(1)}, ...), branch_computations={%region_3.3_spmd, %region_4.4_spmd.clone} | conditional | flops 53850800 | bytes 11276004 | solution.py:136
  211.2 3.6 %fusion.11 = (f32[8,128,64]{1,2,0:T(8,128)S(1)}, f32[8,128,64]{1,2,0:T(8,128)S(1)}, f32[8,128,64]{1,2,0:T(8,128)S(1)}, f32[8,128,64]{1,2,0:T(8,128)S(1)}, f32[8,...) fusion(f32[128]{0:T(128)S(1)} %get-tuple-element.437, ...), kind=kLoop, calls=%fused_computation.9 | loop fusion | flops 3473408 | bytes 2684416 | tf_op jit(solution)/shard_map/while/body/eval_jaxpr/cond/branch_1_fun/jit(_where)/select_n | solution.py:91
  214.8 6.2 %stack.51 = f32[8,8,128,64]{2,0,3,1:T(8,128)} concatenate(f32[1,8,128,64]{2,0,3,1:T(1,128)} %bitcast.229, f32[1,8,128,64]{2,0,3,1:T(1,128)} %bitcast.228, f32[1,8,128,64]{2,0,3,1:T(1,128)} %bitcast.227, f32[1,8,128,64]{2,0,3,1:T(1,128)S(1)} %bitcast.226, f32[1,8,128,64]{2,0,3,1:T(1,128)S(1)} %bitcast.225, f32[1,8,128,64]{2,0,3,1:T(1,128)S(1)} %bitcast.224, ...), dimensions={0} | concatenate | bytes 4194304 | tf_op jit(solution)/shard_map/while/body/eval_jaxpr/cond/branch_1_fun/stack | solution.py:126
  221.0 6.9 %convolution_bitcast_fusion = f32[1,8,8,8,64]{2,3,4,1,0:T(8,128)} fusion(f32[8,8,128,64]{2,0,3,1:T(8,128)} %stack.51, f32[128,8,8,64]{0,2,3,1:T(8,128)} %get-tuple-element.428), kind=kOutput, calls=%fused_computation.4 | convolution fusion | flops 50331648 | bytes 4325376 | tf_op jit(solution)/shard_map/while/body/eval_jaxpr/cond/branch_1_fun/jgkq,kgcq->gcjq/dot_general | solution.py:127
  232.2 18.6 %conditional.4 = (f32[8,128,64]{1,2,0:T(8,128)S(1)}, f32[8,128,64]{1,2,0:T(8,128)S(1)}, f32[1,8,8,8,64]{2,3,4,1,0:T(8,128)}) conditional(s32[]{:T(128)} %convert_element_type.412, (f32[8,128,64]{1,2,0:T(8,128)S(1)}, f32[8,128,64]{1,2,0:T(8,128)S(1)}) %tuple.139, (s32[]{:T(128)}, s32[8]{0:T(128)S(1)}, s32[8,1,1]{0,2,1:T(1,128)S(1)}, ...), branch_computations={%region_3.3_spmd, %region_4.4_spmd.clone} | conditional | flops 53850800 | bytes 11276004 | solution.py:136
  234.0 3.6 %fusion.11 = (f32[8,128,64]{1,2,0:T(8,128)S(1)}, f32[8,128,64]{1,2,0:T(8,128)S(1)}, f32[8,128,64]{1,2,0:T(8,128)S(1)}, f32[8,128,64]{1,2,0:T(8,128)S(1)}, f32[8,...) fusion(f32[128]{0:T(128)S(1)} %get-tuple-element.437, ...), kind=kLoop, calls=%fused_computation.9 | loop fusion | flops 3473408 | bytes 2684416 | tf_op jit(solution)/shard_map/while/body/eval_jaxpr/cond/branch_1_fun/jit(_where)/select_n | solution.py:91
  237.6 6.2 %stack.51 = f32[8,8,128,64]{2,0,3,1:T(8,128)} concatenate(f32[1,8,128,64]{2,0,3,1:T(1,128)} %bitcast.229, f32[1,8,128,64]{2,0,3,1:T(1,128)} %bitcast.228, f32[1,8,128,64]{2,0,3,1:T(1,128)} %bitcast.227, f32[1,8,128,64]{2,0,3,1:T(1,128)S(1)} %bitcast.226, f32[1,8,128,64]{2,0,3,1:T(1,128)S(1)} %bitcast.225, f32[1,8,128,64]{2,0,3,1:T(1,128)S(1)} %bitcast.224, ...), dimensions={0} | concatenate | bytes 4194304 | tf_op jit(solution)/shard_map/while/body/eval_jaxpr/cond/branch_1_fun/stack | solution.py:126
  243.8 6.9 %convolution_bitcast_fusion = f32[1,8,8,8,64]{2,3,4,1,0:T(8,128)} fusion(f32[8,8,128,64]{2,0,3,1:T(8,128)} %stack.51, f32[128,8,8,64]{0,2,3,1:T(8,128)} %get-tuple-element.428), kind=kOutput, calls=%fused_computation.4 | convolution fusion | flops 50331648 | bytes 4325376 | tf_op jit(solution)/shard_map/while/body/eval_jaxpr/cond/branch_1_fun/jgkq,kgcq->gcjq/dot_general | solution.py:127
  250.8 3.1 constant_dynamic-update-slice_fusion.2
  255.0 18.6 %conditional.4 = (f32[8,128,64]{1,2,0:T(8,128)S(1)}, f32[8,128,64]{1,2,0:T(8,128)S(1)}, f32[1,8,8,8,64]{2,3,4,1,0:T(8,128)}) conditional(s32[]{:T(128)} %convert_element_type.412, (f32[8,128,64]{1,2,0:T(8,128)S(1)}, f32[8,128,64]{1,2,0:T(8,128)S(1)}) %tuple.139, (s32[]{:T(128)}, s32[8]{0:T(128)S(1)}, s32[8,1,1]{0,2,1:T(1,128)S(1)}, ...), branch_computations={%region_3.3_spmd, %region_4.4_spmd.clone} | conditional | flops 53850800 | bytes 11276004 | solution.py:136
  256.8 3.6 %fusion.11 = (f32[8,128,64]{1,2,0:T(8,128)S(1)}, f32[8,128,64]{1,2,0:T(8,128)S(1)}, f32[8,128,64]{1,2,0:T(8,128)S(1)}, f32[8,128,64]{1,2,0:T(8,128)S(1)}, f32[8,...) fusion(f32[128]{0:T(128)S(1)} %get-tuple-element.437, ...), kind=kLoop, calls=%fused_computation.9 | loop fusion | flops 3473408 | bytes 2684416 | tf_op jit(solution)/shard_map/while/body/eval_jaxpr/cond/branch_1_fun/jit(_where)/select_n | solution.py:91
  260.4 6.2 %stack.51 = f32[8,8,128,64]{2,0,3,1:T(8,128)} concatenate(f32[1,8,128,64]{2,0,3,1:T(1,128)} %bitcast.229, f32[1,8,128,64]{2,0,3,1:T(1,128)} %bitcast.228, f32[1,8,128,64]{2,0,3,1:T(1,128)} %bitcast.227, f32[1,8,128,64]{2,0,3,1:T(1,128)S(1)} %bitcast.226, f32[1,8,128,64]{2,0,3,1:T(1,128)S(1)} %bitcast.225, f32[1,8,128,64]{2,0,3,1:T(1,128)S(1)} %bitcast.224, ...), dimensions={0} | concatenate | bytes 4194304 | tf_op jit(solution)/shard_map/while/body/eval_jaxpr/cond/branch_1_fun/stack | solution.py:126
  266.7 6.9 %convolution_bitcast_fusion = f32[1,8,8,8,64]{2,3,4,1,0:T(8,128)} fusion(f32[8,8,128,64]{2,0,3,1:T(8,128)} %stack.51, f32[128,8,8,64]{0,2,3,1:T(8,128)} %get-tuple-element.428), kind=kOutput, calls=%fused_computation.4 | convolution fusion | flops 50331648 | bytes 4325376 | tf_op jit(solution)/shard_map/while/body/eval_jaxpr/cond/branch_1_fun/jgkq,kgcq->gcjq/dot_general | solution.py:127
  276.7 11.1 %copy.62 = f32[8,8,8,8,64]{4,3,2,1,0:T(8,128)} copy(f32[8,8,8,8,64]{1,3,4,0,2:T(8,128)} %bitcast.221) | data formatting | bytes 2097152 | tf_op jit(solution)/shard_map/transpose | solution.py:144
  287.8 8.5 %multiply_reduce_fusion = f32[8,8,8]{0,2,1:T(8,128)S(1)} fusion(f32[64]{0:T(128)S(1)} %compare_select_fusion.9, f32[8,8]{1,0:T(8,128)S(1)} %sqrt_multiply_fusion, f32[8,8,8,8,64]{2,3,4,1,0:T(8,128)} %get-tuple-element.216), kind=kLoop, calls=%fused_computation.97 | loop fusion | flops 1048064 | bytes 1051136 | tf_op jit(solution)/shard_map/reduce_sum | solution.py:152
  296.5 45.8 %psum.7 = f32[4,64]{1,0:T(4,128)} all-reduce(f32[4,64]{1,0:T(4,128)S(1)} %broadcast_divide_fusion), channel_id=1, replica_groups=mesh['beta'=16,'grp'=2] {'beta'}, use_global_device_ids=true, to_apply=%region_8.9 | all-reduce | flops 256 | bytes 2048 | tf_op jit(solution)/shard_map/psum | solution.py:179
  342.3 3.3 broadcast_multiply_fusion
  (280 shorter events, 39.6 us)
Async XLA Ops:
  0.6 1.6 copy-start
  18.8 51.5 %all-to-all-start = ((f32[16,1,32768]{2,1,0:T(1,128)}), f32[16,1,32768]{2,1,0:T(1,128)}, u32[]{:S(2)}, u32[]{:S(2)}) async-start(f32[16,1,32768]{2,1,0:T(1,128)} %reshape.2457), calls=%async_computation | async-start | bytes 4194304 | tf_op jit(solution)/shard_map/all_to_all | solution.py:173
  94.1 1.1 copy-start.2
  113.8 3.1 copy-start.3
  116.9 1.1 copy-start.2
  136.7 3.1 copy-start.3
  139.7 1.1 copy-start.2
  159.5 3.1 copy-start.3
  162.6 1.1 copy-start.2
  182.3 3.1 copy-start.3
  185.4 1.1 copy-start.2
  205.1 3.1 copy-start.3
  208.3 1.1 copy-start.2
  228.0 3.1 copy-start.3
  231.1 1.1 copy-start.2
  250.8 3.1 copy-start.3
  253.9 1.1 copy-start.2
  273.6 3.0 copy-start.3
  287.8 8.7 %copy-start.1 = (f32[64]{0:T(128)S(1)}, f32[64]{0:T(128)}, u32[]{:S(2)}) copy-start(f32[64]{0:T(128)} %fusion.87) | copy-start | bytes 772
where the time goes:
time: 351 us; the launch traced here: 346 us
  local copies, waits for them, and re-layouts  117 us (33%)
  other arithmetic  62.1 us (18%)
  matrix products  59.5 us (17%)
  blocking collectives  45.8 us (13%)
  waiting for transfers between devices  38.1 us (11%)
  loops' own time  11.6 us (3%)
  starting transfers between devices  8.4 us (2%)
  between operations  3.57 us (1%)
    dot_general x8, matrix products, compute_block(): jnp.einsum('jgkq,kgcq->gcjq', stacked, weighted, precision=HIGHEST)  55.6 us
    another operation x8, local copies, waits for them, and re-layouts, compute_block(): stacked = jnp.stack(levels, axis=0)  49.9 us
    psum x1, blocking collectives, local(): power = lax.psum(power_part, 'beta')  45.8 us
    all_to_all x1, waiting for transfers between devices, local(): lax.all_to_all(spectrum, 'beta', split_axis=1, concat_axis=0, tiled=True)  38.1 us
    select_n x8, other arithmetic, advance(): renewed = jnp.where(degree == lowest, start_value, recurred)  28.7 us
    dynamic_update_slice x8, local copies, waits for them, and re-layouts, degree_rows(): lax.scan(block_step, (empty_state, empty_state), jnp.arange(block_count,...  24.7 us
    unnamed x7, local copies, waits for them, and re-layouts  15.6 us
    transpose x1, local copies, waits for them, and re-layouts, degree_rows(): jnp.transpose(parts, (1, 2, 0, 3, 4))  11.1 us
  transfers between devices with their start and end apart: 1, of which 1 were waited for; matrix products, arithmetic and copies ran while one was open for 1% of the time, Pallas kernels for 0%

commit v1 on v0

--- a/solution.py
+++ b/solution.py
@@ -4,6 +4,14 @@
 from jax.sharding import PartitionSpec as P
 
 HIGHEST = lax.Precision.HIGHEST
+
+
+def put_pairs_all(message):
+    part_now = jnp.concatenate(
+        lax.all_to_all(jnp.stack(jnp.split(message, lax.axis_size("beta"), 1)), "beta", 0, 0),
+        axis=0,
+    )
+    return part_now
 
 
 def beta_angles(spread):
@@ -170,7 +178,7 @@
         "kfacq,spca->kpsfq", halfway, alpha_table(spread, natural_rows), precision=HIGHEST
     )
     spectrum = spectrum.reshape(local_beta, grid_size, channels, spread)
-    received = lax.all_to_all(spectrum, "beta", split_axis=1, concat_axis=0, tiled=True)
+    received = put_pairs_all(spectrum)
     weighted = received * quadrature(spread)[:, None, None, None]
     owned_rows = lax.dynamic_slice_in_dim(natural_rows, device * row_count, row_count)
     computed = degree_rows(owned_rows, weighted, spread)

time: 351 us -> 401 us (1.14)
  local copies, waits for them, and re-layouts: 117 us -> 169 us
  matrix products: 59.5 us -> 54.4 us
    another operation x0 -> x18, local copies, waits for them, and re-layouts: none -> 51.8 us  [put_pairs_all(): jnp.stack(jnp.split(message, lax.axis_size('beta'), 1))]
    unnamed x7 -> x34, local copies, waits for them, and re-layouts: 15.6 us -> 34.1 us
    another operation x8, local copies, waits for them, and re-layouts: 49.9 us -> 40.8 us  [compute_block(): stacked = jnp.stack(levels, axis=0)]
    reshape x1 -> x0, local copies, waits for them, and re-layouts: 5.57 us -> none  [local(): spectrum = spectrum.reshape(local_beta, grid_size, channels, spread)]
    dot_general x8, matrix products: 55.6 us -> 50.5 us  [compute_block(): jnp.einsum('jgkq,kgcq->gcjq', stacked, weighted, precision=HIGHEST)]
  transfers between devices with their start and end apart: 1 -> 1, of which waited for: 1 -> 1; matrix products, arithmetic and copies ran while one was open for 1% -> 0% of each run, Pallas kernels for 0% -> 0%
where the time goes in v1:
time: 401 us; the launch traced here: 396 us
  local copies, waits for them, and re-layouts  169 us (42%)
  other arithmetic  62.3 us (16%)
  matrix products  54.4 us (14%)
  blocking collectives  45.7 us (11%)
  waiting for transfers between devices  38.9 us (10%)
  loops' own time  14 us (3%)
  starting transfers between devices  8.35 us (2%)
    another operation x18, local copies, waits for them, and re-layouts, put_pairs_all(): jnp.stack(jnp.split(message, lax.axis_size('beta'), 1))  51.8 us
    dot_general x8, matrix products, compute_block(): jnp.einsum('jgkq,kgcq->gcjq', stacked, weighted, precision=HIGHEST)  50.5 us
    psum x1, blocking collectives, local(): power = lax.psum(power_part, 'beta')  45.7 us
    another operation x8, local copies, waits for them, and re-layouts, compute_block(): stacked = jnp.stack(levels, axis=0)  40.8 us
    all_to_all x1, waiting for transfers between devices, put_pairs_all(): lax.all_to_all(jnp.stack(jnp.split(message, lax.axis_size('beta'), 1)), '...  38.9 us
    unnamed x34, local copies, waits for them, and re-layouts  34.1 us
    select_n x8, other arithmetic, advance(): renewed = jnp.where(degree == lowest, start_value, recurred)  28.5 us
    dynamic_update_slice x8, local copies, waits for them, and re-layouts, degree_rows(): lax.scan(block_step, (empty_state, empty_state), jnp.arange(block_count,...  24.6 us
  transfers between devices with their start and end apart: 1, of which 1 were waited for; matrix products, arithmetic and copies ran while one was open for 0% of the time, Pallas kernels for 0%

profile of v1, /device:TPU:0, one launch (start us, length us, event | category | flops | bytes accessed | tf_op | source)
XLA Modules:
  0.0 395.9 jit_solution(16588423047978105721)
XLA Ops:
  6.4 13.4 %slice_bitcast_fusion = (f32[1,8,8,8,64]{2,4,3,1,0:T(8,128)}, f32[1,8,8,8,64]{2,4,3,1,0:T(8,128)}, f32[1,8,8,8,64]{2,4,3,1,0:T(8,128)}, f32[1,8,8,8,64]{2,4,3,1,...) fusion(f32[8,128,8,64]{1,3,2,0:T(8,128)S(1)} %bitcast.248), kind=kLoop, calls=%fused_computation.99 | loop fusion | bytes 4194304 | tf_op jit(solution)/shard_map/stack | solution.py:11
  76.6 5.5 %reshape.2461 = f32[16,1,32768]{2,1,0:T(1,128)} reshape(f32[16,8,8,8,64]{4,3,2,1,0:T(8,128)} %constant_dynamic-update-slice_fusion.1) | data formatting | bytes 4194304
  82.1 8.3 %all-to-all-start = ((f32[16,1,32768]{2,1,0:T(1,128)}), f32[16,1,32768]{2,1,0:T(1,128)S(1)}, u32[]{:S(2)}, u32[]{:S(2)}) async-start(f32[16,1,32768]{2,1,0:T(1,128)} %reshape.2461), calls=%async_computation | async-start | bytes 4194304 | tf_op jit(solution)/shard_map/all_to_all | solution.py:11
  94.6 38.9 %all-to-all-done = f32[16,1,32768]{2,1,0:T(1,128)S(1)} async-done(((f32[16,1,32768]{2,1,0:T(1,128)}), f32[16,1,32768]{2,1,0:T(1,128)S(1)}, u32[]{:S(2)}, u32[]{:S(2)}) %all-to-all-start) | async-done | bytes 2097184 | tf_op jit(solution)/shard_map/all_to_all | solution.py:11
  135.4 7.3 %reduce.3 = f32[16,32768]{1,0:T(8,128)S(1)} reduce(f32[16,1,32768]{2,1,0:T(1,128)} %copy-done.5, f32[]{:T(128)} %broadcast.2681), dimensions={1}, to_apply=%all_to_all.3.reduce_sub_computation | reduce | bytes 4194308 | tf_op jit(solution)/shard_map/all_to_all | solution.py:11
  145.6 4.5 %bitcast_multiply_fusion = f32[128,8,8,64]{3,2,1,0:T(8,128)} fusion(f32[16,8,8,8,64]{4,3,2,1,0:T(8,128)} %reshape.2462, f32[128]{0:T(128)S(1)} %multiply_multiply_fusion), kind=kLoop, calls=%fused_computation.98 | loop fusion | flops 524288 | bytes 4194816 | tf_op jit(solution)/shard_map/mul | solution.py:182
  150.2 5.0 %copy.114 = f32[128,8,8,64]{0,2,3,1:T(8,128)} copy(f32[128,8,8,64]{3,2,1,0:T(8,128)} %bitcast_multiply_fusion) | data formatting | bytes 4194304
  155.2 171.6 %while.16 = (s32[]{:T(128)}, f32[8,128,64]{1,2,0:T(8,128)S(1)}, f32[8,128,64]{1,2,0:T(8,128)S(1)}, f32[8,8,8,8,64]{2,3,4,1,0:T(8,128)}, s32[8]{0:T(128)S(1)}, /*...) while((s32[]{:T(128)}, f32[8,128,64]{1,2,0:T(8,128)S(1)}, ...), condition=%wide.region_5.6_spmd.clone.clone, body=%wide.region_2.5_spmd.clone.clone.sunk | while | flops 53850804 | bytes 15474075 | solution.py:149
  156.9 17.0 %conditional.4 = (f32[8,128,64]{1,2,0:T(8,128)S(1)}, f32[8,128,64]{1,2,0:T(8,128)S(1)}, f32[1,8,8,8,64]{2,3,4,1,0:T(8,128)}) conditional(s32[]{:T(128)} %convert_element_type.412, (f32[8,128,64]{1,2,0:T(8,128)S(1)}, f32[8,128,64]{1,2,0:T(8,128)S(1)}) %tuple.154, (s32[]{:T(128)}, s32[8]{0:T(128)S(1)}, s32[8,1,1]{0,2,1:T(1,128)S(1)}, ...), branch_computations={%region_3.3_spmd, %region_4.4_spmd.clone} | conditional | flops 53850800 | bytes 11276004 | solution.py:144
  158.9 3.6 fusion.11
  162.4 5.1 %stack.119 = f32[8,8,128,64]{2,0,3,1:T(8,128)S(1)} concatenate(f32[1,8,128,64]{2,0,3,1:T(1,128)} %bitcast.257, f32[1,8,128,64]{2,0,3,1:T(1,128)} %bitcast.256, f32[1,8,128,64]{2,0,3,1:T(1,128)} %bitcast.255, f32[1,8,128,64]{2,0,3,1:T(1,128)S(1)} %bitcast.254, f32[1,8,128,64]{2,0,3,1:T(1,128)S(1)} %bitcast.253, f32[1,8,128,64]{2,0,3,1:T(1,128)S(1)} %bitcast.252, ...), dimensions={0} | concatenate | bytes 4194304 | tf_op jit(solution)/shard_map/while/body/eval_jaxpr/cond/branch_1_fun/stack | solution.py:134
  167.5 6.3 %convolution_bitcast_fusion = f32[1,8,8,8,64]{2,3,4,1,0:T(8,128)} fusion(f32[8,8,128,64]{2,0,3,1:T(8,128)S(1)} %stack.119, f32[128,8,8,64]{0,2,3,1:T(8,128)} %get-tuple-element.428), kind=kOutput, calls=%fused_computation.4 | convolution fusion | flops 50331648 | bytes 4325376 | tf_op jit(solution)/shard_map/while/body/eval_jaxpr/cond/branch_1_fun/jgkq,kgcq->gcjq/dot_general | solution.py:135
  178.3 17.0 %conditional.4 = (f32[8,128,64]{1,2,0:T(8,128)S(1)}, f32[8,128,64]{1,2,0:T(8,128)S(1)}, f32[1,8,8,8,64]{2,3,4,1,0:T(8,128)}) conditional(s32[]{:T(128)} %convert_element_type.412, (f32[8,128,64]{1,2,0:T(8,128)S(1)}, f32[8,128,64]{1,2,0:T(8,128)S(1)}) %tuple.154, (s32[]{:T(128)}, s32[8]{0:T(128)S(1)}, s32[8,1,1]{0,2,1:T(1,128)S(1)}, ...), branch_computations={%region_3.3_spmd, %region_4.4_spmd.clone} | conditional | flops 53850800 | bytes 11276004 | solution.py:144
  180.3 3.6 fusion.11
  183.8 5.1 %stack.119 = f32[8,8,128,64]{2,0,3,1:T(8,128)S(1)} concatenate(f32[1,8,128,64]{2,0,3,1:T(1,128)} %bitcast.257, f32[1,8,128,64]{2,0,3,1:T(1,128)} %bitcast.256, f32[1,8,128,64]{2,0,3,1:T(1,128)} %bitcast.255, f32[1,8,128,64]{2,0,3,1:T(1,128)S(1)} %bitcast.254, f32[1,8,128,64]{2,0,3,1:T(1,128)S(1)} %bitcast.253, f32[1,8,128,64]{2,0,3,1:T(1,128)S(1)} %bitcast.252, ...), dimensions={0} | concatenate | bytes 4194304 | tf_op jit(solution)/shard_map/while/body/eval_jaxpr/cond/branch_1_fun/stack | solution.py:134
  188.9 6.3 %convolution_bitcast_fusion = f32[1,8,8,8,64]{2,3,4,1,0:T(8,128)} fusion(f32[8,8,128,64]{2,0,3,1:T(8,128)S(1)} %stack.119, f32[128,8,8,64]{0,2,3,1:T(8,128)} %get-tuple-element.428), kind=kOutput, calls=%fused_computation.4 | convolution fusion | flops 50331648 | bytes 4325376 | tf_op jit(solution)/shard_map/while/body/eval_jaxpr/cond/branch_1_fun/jgkq,kgcq->gcjq/dot_general | solution.py:135
  199.7 17.0 %conditional.4 = (f32[8,128,64]{1,2,0:T(8,128)S(1)}, f32[8,128,64]{1,2,0:T(8,128)S(1)}, f32[1,8,8,8,64]{2,3,4,1,0:T(8,128)}) conditional(s32[]{:T(128)} %convert_element_type.412, (f32[8,128,64]{1,2,0:T(8,128)S(1)}, f32[8,128,64]{1,2,0:T(8,128)S(1)}) %tuple.154, (s32[]{:T(128)}, s32[8]{0:T(128)S(1)}, s32[8,1,1]{0,2,1:T(1,128)S(1)}, ...), branch_computations={%region_3.3_spmd, %region_4.4_spmd.clone} | conditional | flops 53850800 | bytes 11276004 | solution.py:144
  201.6 3.6 fusion.11
  205.2 5.1 %stack.119 = f32[8,8,128,64]{2,0,3,1:T(8,128)S(1)} concatenate(f32[1,8,128,64]{2,0,3,1:T(1,128)} %bitcast.257, f32[1,8,128,64]{2,0,3,1:T(1,128)} %bitcast.256, f32[1,8,128,64]{2,0,3,1:T(1,128)} %bitcast.255, f32[1,8,128,64]{2,0,3,1:T(1,128)S(1)} %bitcast.254, f32[1,8,128,64]{2,0,3,1:T(1,128)S(1)} %bitcast.253, f32[1,8,128,64]{2,0,3,1:T(1,128)S(1)} %bitcast.252, ...), dimensions={0} | concatenate | bytes 4194304 | tf_op jit(solution)/shard_map/while/body/eval_jaxpr/cond/branch_1_fun/stack | solution.py:134
  210.3 6.3 %convolution_bitcast_fusion = f32[1,8,8,8,64]{2,3,4,1,0:T(8,128)} fusion(f32[8,8,128,64]{2,0,3,1:T(8,128)S(1)} %stack.119, f32[128,8,8,64]{0,2,3,1:T(8,128)} %get-tuple-element.428), kind=kOutput, calls=%fused_computation.4 | convolution fusion | flops 50331648 | bytes 4325376 | tf_op jit(solution)/shard_map/while/body/eval_jaxpr/cond/branch_1_fun/jgkq,kgcq->gcjq/dot_general | solution.py:135
  216.6 3.1 constant_dynamic-update-slice_fusion.18
  221.1 17.0 %conditional.4 = (f32[8,128,64]{1,2,0:T(8,128)S(1)}, f32[8,128,64]{1,2,0:T(8,128)S(1)}, f32[1,8,8,8,64]{2,3,4,1,0:T(8,128)}) conditional(s32[]{:T(128)} %convert_element_type.412, (f32[8,128,64]{1,2,0:T(8,128)S(1)}, f32[8,128,64]{1,2,0:T(8,128)S(1)}) %tuple.154, (s32[]{:T(128)}, s32[8]{0:T(128)S(1)}, s32[8,1,1]{0,2,1:T(1,128)S(1)}, ...), branch_computations={%region_3.3_spmd, %region_4.4_spmd.clone} | conditional | flops 53850800 | bytes 11276004 | solution.py:144
  223.1 3.6 fusion.11
  226.6 5.1 %stack.119 = f32[8,8,128,64]{2,0,3,1:T(8,128)S(1)} concatenate(f32[1,8,128,64]{2,0,3,1:T(1,128)} %bitcast.257, f32[1,8,128,64]{2,0,3,1:T(1,128)} %bitcast.256, f32[1,8,128,64]{2,0,3,1:T(1,128)} %bitcast.255, f32[1,8,128,64]{2,0,3,1:T(1,128)S(1)} %bitcast.254, f32[1,8,128,64]{2,0,3,1:T(1,128)S(1)} %bitcast.253, f32[1,8,128,64]{2,0,3,1:T(1,128)S(1)} %bitcast.252, ...), dimensions={0} | concatenate | bytes 4194304 | tf_op jit(solution)/shard_map/while/body/eval_jaxpr/cond/branch_1_fun/stack | solution.py:134
  231.7 6.3 %convolution_bitcast_fusion = f32[1,8,8,8,64]{2,3,4,1,0:T(8,128)} fusion(f32[8,8,128,64]{2,0,3,1:T(8,128)S(1)} %stack.119, f32[128,8,8,64]{0,2,3,1:T(8,128)} %get-tuple-element.428), kind=kOutput, calls=%fused_computation.4 | convolution fusion | flops 50331648 | bytes 4325376 | tf_op jit(solution)/shard_map/while/body/eval_jaxpr/cond/branch_1_fun/jgkq,kgcq->gcjq/dot_general | solution.py:135
  238.0 3.1 constant_dynamic-update-slice_fusion.18
  242.5 17.0 %conditional.4 = (f32[8,128,64]{1,2,0:T(8,128)S(1)}, f32[8,128,64]{1,2,0:T(8,128)S(1)}, f32[1,8,8,8,64]{2,3,4,1,0:T(8,128)}) conditional(s32[]{:T(128)} %convert_element_type.412, (f32[8,128,64]{1,2,0:T(8,128)S(1)}, f32[8,128,64]{1,2,0:T(8,128)S(1)}) %tuple.154, (s32[]{:T(128)}, s32[8]{0:T(128)S(1)}, s32[8,1,1]{0,2,1:T(1,128)S(1)}, ...), branch_computations={%region_3.3_spmd, %region_4.4_spmd.clone} | conditional | flops 53850800 | bytes 11276004 | solution.py:144
  244.5 3.6 fusion.11
  248.1 5.1 %stack.119 = f32[8,8,128,64]{2,0,3,1:T(8,128)S(1)} concatenate(f32[1,8,128,64]{2,0,3,1:T(1,128)} %bitcast.257, f32[1,8,128,64]{2,0,3,1:T(1,128)} %bitcast.256, f32[1,8,128,64]{2,0,3,1:T(1,128)} %bitcast.255, f32[1,8,128,64]{2,0,3,1:T(1,128)S(1)} %bitcast.254, f32[1,8,128,64]{2,0,3,1:T(1,128)S(1)} %bitcast.253, f32[1,8,128,64]{2,0,3,1:T(1,128)S(1)} %bitcast.252, ...), dimensions={0} | concatenate | bytes 4194304 | tf_op jit(solution)/shard_map/while/body/eval_jaxpr/cond/branch_1_fun/stack | solution.py:134
  253.2 6.3 %convolution_bitcast_fusion = f32[1,8,8,8,64]{2,3,4,1,0:T(8,128)} fusion(f32[8,8,128,64]{2,0,3,1:T(8,128)S(1)} %stack.119, f32[128,8,8,64]{0,2,3,1:T(8,128)} %get-tuple-element.428), kind=kOutput, calls=%fused_computation.4 | convolution fusion | flops 50331648 | bytes 4325376 | tf_op jit(solution)/shard_map/while/body/eval_jaxpr/cond/branch_1_fun/jgkq,kgcq->gcjq/dot_general | solution.py:135
  259.5 3.1 constant_dynamic-update-slice_fusion.18
  264.0 17.0 %conditional.4 = (f32[8,128,64]{1,2,0:T(8,128)S(1)}, f32[8,128,64]{1,2,0:T(8,128)S(1)}, f32[1,8,8,8,64]{2,3,4,1,0:T(8,128)}) conditional(s32[]{:T(128)} %convert_element_type.412, (f32[8,128,64]{1,2,0:T(8,128)S(1)}, f32[8,128,64]{1,2,0:T(8,128)S(1)}) %tuple.154, (s32[]{:T(128)}, s32[8]{0:T(128)S(1)}, s32[8,1,1]{0,2,1:T(1,128)S(1)}, ...), branch_computations={%region_3.3_spmd, %region_4.4_spmd.clone} | conditional | flops 53850800 | bytes 11276004 | solution.py:144
  266.0 3.6 fusion.11
  269.5 5.1 %stack.119 = f32[8,8,128,64]{2,0,3,1:T(8,128)S(1)} concatenate(f32[1,8,128,64]{2,0,3,1:T(1,128)} %bitcast.257, f32[1,8,128,64]{2,0,3,1:T(1,128)} %bitcast.256, f32[1,8,128,64]{2,0,3,1:T(1,128)} %bitcast.255, f32[1,8,128,64]{2,0,3,1:T(1,128)S(1)} %bitcast.254, f32[1,8,128,64]{2,0,3,1:T(1,128)S(1)} %bitcast.253, f32[1,8,128,64]{2,0,3,1:T(1,128)S(1)} %bitcast.252, ...), dimensions={0} | concatenate | bytes 4194304 | tf_op jit(solution)/shard_map/while/body/eval_jaxpr/cond/branch_1_fun/stack | solution.py:134
  274.6 6.3 %convolution_bitcast_fusion = f32[1,8,8,8,64]{2,3,4,1,0:T(8,128)} fusion(f32[8,8,128,64]{2,0,3,1:T(8,128)S(1)} %stack.119, f32[128,8,8,64]{0,2,3,1:T(8,128)} %get-tuple-element.428), kind=kOutput, calls=%fused_computation.4 | convolution fusion | flops 50331648 | bytes 4325376 | tf_op jit(solution)/shard_map/while/body/eval_jaxpr/cond/branch_1_fun/jgkq,kgcq->gcjq/dot_general | solution.py:135
  281.0 3.1 constant_dynamic-update-slice_fusion.18
  285.4 17.0 %conditional.4 = (f32[8,128,64]{1,2,0:T(8,128)S(1)}, f32[8,128,64]{1,2,0:T(8,128)S(1)}, f32[1,8,8,8,64]{2,3,4,1,0:T(8,128)}) conditional(s32[]{:T(128)} %convert_element_type.412, (f32[8,128,64]{1,2,0:T(8,128)S(1)}, f32[8,128,64]{1,2,0:T(8,128)S(1)}) %tuple.154, (s32[]{:T(128)}, s32[8]{0:T(128)S(1)}, s32[8,1,1]{0,2,1:T(1,128)S(1)}, ...), branch_computations={%region_3.3_spmd, %region_4.4_spmd.clone} | conditional | flops 53850800 | bytes 11276004 | solution.py:144
  287.4 3.6 fusion.11
  291.0 5.1 %stack.119 = f32[8,8,128,64]{2,0,3,1:T(8,128)S(1)} concatenate(f32[1,8,128,64]{2,0,3,1:T(1,128)} %bitcast.257, f32[1,8,128,64]{2,0,3,1:T(1,128)} %bitcast.256, f32[1,8,128,64]{2,0,3,1:T(1,128)} %bitcast.255, f32[1,8,128,64]{2,0,3,1:T(1,128)S(1)} %bitcast.254, f32[1,8,128,64]{2,0,3,1:T(1,128)S(1)} %bitcast.253, f32[1,8,128,64]{2,0,3,1:T(1,128)S(1)} %bitcast.252, ...), dimensions={0} | concatenate | bytes 4194304 | tf_op jit(solution)/shard_map/while/body/eval_jaxpr/cond/branch_1_fun/stack | solution.py:134
  296.1 6.3 %convolution_bitcast_fusion = f32[1,8,8,8,64]{2,3,4,1,0:T(8,128)} fusion(f32[8,8,128,64]{2,0,3,1:T(8,128)S(1)} %stack.119, f32[128,8,8,64]{0,2,3,1:T(8,128)} %get-tuple-element.428), kind=kOutput, calls=%fused_computation.4 | convolution fusion | flops 50331648 | bytes 4325376 | tf_op jit(solution)/shard_map/while/body/eval_jaxpr/cond/branch_1_fun/jgkq,kgcq->gcjq/dot_general | solution.py:135
  306.8 17.0 %conditional.4 = (f32[8,128,64]{1,2,0:T(8,128)S(1)}, f32[8,128,64]{1,2,0:T(8,128)S(1)}, f32[1,8,8,8,64]{2,3,4,1,0:T(8,128)}) conditional(s32[]{:T(128)} %convert_element_type.412, (f32[8,128,64]{1,2,0:T(8,128)S(1)}, f32[8,128,64]{1,2,0:T(8,128)S(1)}) %tuple.154, (s32[]{:T(128)}, s32[8]{0:T(128)S(1)}, s32[8,1,1]{0,2,1:T(1,128)S(1)}, ...), branch_computations={%region_3.3_spmd, %region_4.4_spmd.clone} | conditional | flops 53850800 | bytes 11276004 | solution.py:144
  308.8 3.6 fusion.11
  312.4 5.1 %stack.119 = f32[8,8,128,64]{2,0,3,1:T(8,128)S(1)} concatenate(f32[1,8,128,64]{2,0,3,1:T(1,128)} %bitcast.257, f32[1,8,128,64]{2,0,3,1:T(1,128)} %bitcast.256, f32[1,8,128,64]{2,0,3,1:T(1,128)} %bitcast.255, f32[1,8,128,64]{2,0,3,1:T(1,128)S(1)} %bitcast.254, f32[1,8,128,64]{2,0,3,1:T(1,128)S(1)} %bitcast.253, f32[1,8,128,64]{2,0,3,1:T(1,128)S(1)} %bitcast.252, ...), dimensions={0} | concatenate | bytes 4194304 | tf_op jit(solution)/shard_map/while/body/eval_jaxpr/cond/branch_1_fun/stack | solution.py:134
  317.5 6.3 %convolution_bitcast_fusion = f32[1,8,8,8,64]{2,3,4,1,0:T(8,128)} fusion(f32[8,8,128,64]{2,0,3,1:T(8,128)S(1)} %stack.119, f32[128,8,8,64]{0,2,3,1:T(8,128)} %get-tuple-element.428), kind=kOutput, calls=%fused_computation.4 | convolution fusion | flops 50331648 | bytes 4325376 | tf_op jit(solution)/shard_map/while/body/eval_jaxpr/cond/branch_1_fun/jgkq,kgcq->gcjq/dot_general | solution.py:135
  326.9 11.1 %copy.115 = f32[8,8,8,8,64]{4,3,2,1,0:T(8,128)} copy(f32[8,8,8,8,64]{1,3,4,0,2:T(8,128)} %bitcast.249) | data formatting | bytes 2097152 | tf_op jit(solution)/shard_map/transpose | solution.py:152
  338.0 8.7 %multiply_reduce_fusion = f32[8,8,8]{0,2,1:T(8,128)S(1)} fusion(f32[64]{0:T(128)S(1)} %compare_select_fusion.9, f32[8,8]{1,0:T(8,128)S(1)} %sqrt_multiply_fusion, f32[8,8,8,8,64]{2,3,4,1,0:T(8,128)} %get-tuple-element.216), kind=kLoop, calls=%fused_computation.97 | loop fusion | flops 1048064 | bytes 1051136 | tf_op jit(solution)/shard_map/reduce_sum | solution.py:160
  346.8 45.7 %psum.7 = f32[4,64]{1,0:T(4,128)} all-reduce(f32[4,64]{1,0:T(4,128)S(1)} %broadcast_divide_fusion), channel_id=1, replica_groups=mesh['beta'=16,'grp'=2] {'beta'}, use_global_device_ids=true, to_apply=%region_8.9 | all-reduce | flops 256 | bytes 2048 | tf_op jit(solution)/shard_map/psum | solution.py:187
  392.6 3.3 broadcast_multiply_fusion
  (291 shorter events, 94.5 us)
Async XLA Ops:
  0.6 1.6 copy-start
  22.7 11.7 %copy-start.4 = (f32[1,8,8,8,64]{2,4,3,1,0:T(8,128)S(1)}, f32[1,8,8,8,64]{2,4,3,1,0:T(8,128)}, u32[]{:S(2)}) copy-start(f32[1,8,8,8,64]{2,4,3,1,0:T(8,128)} %get-tuple-element.583) | copy-start | bytes 393220
  35.7 11.7 %copy-start.3 = (f32[1,8,8,8,64]{2,4,3,1,0:T(8,128)S(1)}, f32[1,8,8,8,64]{2,4,3,1,0:T(8,128)}, u32[]{:S(2)}) copy-start(f32[1,8,8,8,64]{2,4,3,1,0:T(8,128)} %get-tuple-element.578) | copy-start | bytes 393220
  48.7 8.9 %copy-start.2 = (f32[1,8,8,8,64]{2,4,3,1,0:T(8,128)S(1)}, f32[1,8,8,8,64]{2,4,3,1,0:T(8,128)}, u32[]{:S(2)}) copy-start(f32[1,8,8,8,64]{2,4,3,1,0:T(8,128)} %get-tuple-element.573) | copy-start | bytes 393220
  58.2 13.4 %copy-start.7 = (f32[1,8,8,8,64]{4,3,2,1,0:T(8,128)S(1)}, f32[1,8,8,8,64]{4,3,2,1,0:T(8,128)}, u32[]{:S(2)}) copy-start(f32[1,8,8,8,64]{4,3,2,1,0:T(8,128)} %copy.107) | copy-start | bytes 393220
  58.2 14.1 %copy-start.6 = (f32[1,8,8,8,64]{4,3,2,1,0:T(8,128)S(1)}, f32[1,8,8,8,64]{4,3,2,1,0:T(8,128)}, u32[]{:S(2)}) copy-start(f32[1,8,8,8,64]{4,3,2,1,0:T(8,128)} %copy.108) | copy-start | bytes 393220
  82.1 51.4 %all-to-all-start = ((f32[16,1,32768]{2,1,0:T(1,128)}), f32[16,1,32768]{2,1,0:T(1,128)S(1)}, u32[]{:S(2)}, u32[]{:S(2)}) async-start(f32[16,1,32768]{2,1,0:T(1,128)} %reshape.2461), calls=%async_computation | async-start | bytes 4194304 | tf_op jit(solution)/shard_map/all_to_all | solution.py:11
  133.5 1.3 copy-start.5
  338.0 57.9 %copy-start.1 = (f32[8,4,128,128]{3,2,1,0:T(8,128)S(1)}, f32[8,4,128,128]{3,2,1,0:T(8,128)}, u32[]{:S(2)}) copy-start(f32[8,4,128,128]{3,2,1,0:T(8,128)} %param.5) | copy-start | bytes 6291460
